TPU v7x, 512 devices: a 4x2x32 block of a 4x8x32 slice. The times are simulated.
512 devices in a mesh: groups: 2 (over y), seq: 32 (over z), tp: 8 (over x, core).
Axes of the slice: x: 4, y: 2, z: 32, core: 2. Of those that a mesh axis runs over, the one named last changes fastest.
The devices are a block of a 4x8x32 slice.
Arguments:
- prompt_kv: bfloat16 [32768, 64, 128], P(('groups', 'seq', 'tp')), parts along dimension 0, may hold values from -6 to 6
- prompt_length: int32 [2], P('groups'), parts along dimension 0, may hold values from 8192 to 16384
- queries: bfloat16 [16, 4096], P('groups'), parts along dimension 0, may hold values from -6 to 6
- new_kv: bfloat16 [16, 16, 2, 128], P('groups'), parts along dimension 0, may hold values from -6 to 6
- k_cache: bfloat16 [256, 8192, 128], P(('groups', 'seq'), 'tp'), parts along dimension 0, may hold values from -6 to 6
- v_cache: bfloat16 [256, 8192, 128], P(('groups', 'seq'), 'tp'), parts along dimension 0, may hold values from -6 to 6
- lengths: int32 [16], P('groups'), parts along dimension 0, may hold values from 4097 to 8192
- slots: int32 [16], P('groups'), parts along dimension 0, may hold values from 0 to 7, each once
Outputs:
- prompt_owned: bfloat16 [32768, 64, 128], P(('groups', 'tp'), 'seq'), parts along dimension 0
- attended: bfloat16 [256, 256], P(('groups', 'seq')), parts along dimension 0
There are 2 independent parts, one for each index of `groups`. A program takes and returns all parts, laid end to end along the dimension named above; each array names one. Nothing has to cross between parts.
Inputs may be any that keep to these rules, and one draw needn't show every extreme that they name: `slots`: each slot once.
All inputs are finite; a program needn't handle non-finite values.
Results may differ from a plain program's by a relative error of at most 0.0028.
Values may be sent and summed in bfloat16 or wider, within the bound.
A program may use at most 64 MiB of HBM per device.

v0:
```python
import jax
import jax.numpy as jnp
from jax import lax
from jax.sharding import PartitionSpec as P

query_scale = 168.0 ** (-0.5)
negative = -1e30


def collected_together(shard, axis):
    leaves = jax.tree.leaves(shard)
    sequence = sorted(range(len(leaves)), key=lambda k: -leaves[k].size)
    width = (1, *leaves[sequence[0]].shape)[-1]
    lines = [
        jnp.pad(leaves[k].reshape(-1), (0, -leaves[k].size % width)).reshape(-1, width)
        for k in sequence
    ]
    both, at, found = (lax.all_gather(jnp.concatenate(lines), axis), 0, {})
    for k, line in zip(sequence, lines):
        section = both[:, at : at + len(line)].reshape(len(both), -1)
        found[k] = section[:, : leaves[k].size].reshape(-1, *leaves[k].shape)
        at += len(line)
    numbers = iter(range(len(leaves)))
    return jax.tree.map(lambda _: found[next(numbers)], shard)


def joined(shard, axis, combine):
    everything = collected_together(shard, axis)
    leading = jax.tree.map(lambda part: part[0], everything)

    def step(k, so_far):
        return combine(so_far, jax.tree.map(lambda part: part[k], everything))

    return lax.fori_loop(1, lax.axis_size(axis), step, leading)


def combine_parts(first, second):
    upper = jnp.maximum(first[0], second[0])
    scale_one = jnp.exp(first[0] - upper)
    scale_two = jnp.exp(second[0] - upper)
    total = first[1] * scale_one + second[1] * scale_two
    summed = first[2] * scale_one[..., None] + second[2] * scale_two[..., None]
    return (upper, total, summed)


def per_device(prompt_kv, prompt_length, queries, new_kv, k_cache, v_cache, lengths, slots):
    block = prompt_kv.shape[0]
    offset = (lax.axis_index("seq") * lax.axis_size("tp") + lax.axis_index("tp")) * block
    position = offset + jnp.arange(block, dtype=jnp.int32)
    kept = jnp.where(
        (position < prompt_length[0])[:, None, None], prompt_kv, jnp.zeros_like(prompt_kv)
    )
    prompt_owned = lax.all_to_all(kept, "seq", split_axis=1, concat_axis=0, tiled=True)
    resident = lengths.shape[0]
    pair_rows = k_cache.shape[0]
    span = k_cache.shape[1]
    width = k_cache.shape[2]
    heads = new_kv.shape[1]
    group = queries.shape[1] // (heads * width)
    rows = lax.axis_index("seq") * pair_rows + jnp.arange(pair_rows, dtype=jnp.int32)
    head_of = rows // resident
    slot_of = rows % resident
    match = slots[None, :] == slot_of[:, None]
    sequence = jnp.sum(jnp.where(match, jnp.arange(resident, dtype=jnp.int32)[None, :], 0), axis=1)
    grouped = queries.reshape(resident, heads, group, width)
    query_rows = grouped[sequence, head_of]
    own = new_kv[sequence, head_of]
    own_key = own[:, 0]
    own_value = own[:, 1].astype(jnp.float32)
    live_len = lengths[sequence]
    scores = (
        jnp.einsum("rgd,rpd->rgp", query_rows, k_cache, preferred_element_type=jnp.float32)
        * query_scale
    )
    own_score = (
        jnp.einsum("rgd,rd->rg", query_rows, own_key, preferred_element_type=jnp.float32)
        * query_scale
    )
    cache_pos = lax.axis_index("tp") * span + jnp.arange(span, dtype=jnp.int32)
    live = cache_pos[None, None, :] < live_len[:, None, None]
    masked = jnp.where(live, scores, negative)
    local_top = jnp.max(masked, axis=2)
    weights = jnp.where(live, jnp.exp(masked - local_top[..., None]), 0.0)
    partial_value = jnp.einsum(
        "rgp,rpd->rgd", weights.astype(jnp.bfloat16), v_cache, preferred_element_type=jnp.float32
    )
    upper, total, summed = joined(
        (local_top, jnp.sum(weights, axis=2), partial_value), "tp", combine_parts
    )
    overall = jnp.maximum(upper, own_score)
    rescale = jnp.exp(upper - overall)
    own_weight = jnp.exp(own_score - overall)
    total = total * rescale + own_weight
    summed = summed * rescale[..., None] + own_weight[..., None] * own_value[:, None, :]
    attended = (summed / total[..., None]).astype(jnp.bfloat16).reshape(pair_rows, group * width)
    return (prompt_owned, attended)


def solution(mesh):
    in_specs = (
        P(("groups", "seq", "tp"), None, None),
        P("groups"),
        P("groups", None),
        P("groups", None, None, None),
        P(("groups", "seq"), "tp", None),
        P(("groups", "seq"), "tp", None),
        P("groups"),
        P("groups"),
    )
    out_specs = (P(("groups", "tp"), "seq", None), P(("groups", "seq"), None))
    return jax.shard_map(
        per_device, mesh=mesh, in_specs=in_specs, out_specs=out_specs, check_vma=False
    )
```

profile of v0, /device:TPU:33, one launch (start us, length us, event | category | flops | bytes accessed | tf_op | source)
XLA Modules:
  0.0 157.3 jit_solution(15945082994965442945)
XLA Ops:
  1.4 2.9 %copy_select_fusion = bf16[64,64,128]{2,0,1:T(8,128)(2,1)} fusion(bf16[64,64,128]{2,1,0:T(8,128)(2,1)} %param.10, pred[64]{0:T(512)(128)(4,1)S(1)} %add_compare_fusion), kind=kLoop, calls=%fused_computation.14 | loop fusion | flops 524288 | bytes 2097216 | tf_op jit(solution)/shard_map/jit(_where)/select_n | solution.py:50
  4.3 46.4 %all-to-all-start = ((bf16[64,64,128]{2,0,1:T(8,128)(2,1)}), bf16[64,64,128]{2,0,1:T(8,128)(2,1)S(1)}, u32[]{:S(2)}, u32[]{:S(2)}) async-start(bf16[64,64,128]{2,0,1:T(8,128)(2,1)} %copy_select_fusion), calls=%async_computation | async-start | bytes 2097152 | tf_op jit(solution)/shard_map/all_to_all | solution.py:53
  50.9 0.2 select_reduce_fusion
  51.1 0.6 gather_fusion.1
  51.7 0.6 gather_fusion
  52.4 0.5 fusion.23
  53.0 0.2 fusion.6
  53.3 0.3 fusion.4
  53.6 14.3 %all-gather.1 = f32[8,10,128]{2,1,0:T(8,128)S(1)} all-gather(f32[1,10,128]{2,1,0:T(8,128)S(1)} %maximum_bitcast_fusion), channel_id=2, replica_groups=mesh['groups'=2,'seq'=32,'tp'=8] {'tp'}, dimensions={0}, use_global_device_ids=true | all-gather | bytes 46080 | tf_op jit(solution)/shard_map/all_gather | solution.py:18
  67.9 0.6 copy-done.2
  68.5 0.1 copy.61
  68.6 0.1 slice_reduce_fusion.1
  68.8 0.1 copy.52
  68.9 0.1 copy.62
  69.0 0.1 slice_reduce_fusion
  69.2 0.1 copy.53
  69.3 0.1 copy.54
  69.5 1.4 gather_fusion.2
  70.9 0.1 fusion.8
  71.0 0.1 copy.60
  71.1 2.1 %while.19 = (s32[]{:T(128)}, f32[4,2]{0,1:T(2,128)S(1)}, f32[4,2]{0,1:T(2,128)S(1)}, f32[4,2,128]{2,1,0:T(2,128)S(1)}, f32[8,4,2]{1,2,0:T(2,128)S(1)}, /*index=5...) while((s32[]{:T(128)}, f32[4,2]{0,1:T(2,128)S(1)}, ...), condition=%wide.region_4.5_spmd, body=%wide.region_3.4_spmd.sunk | while | flops 3125 | bytes 12887 | solution.py:34
  71.4 0.1 copy.69
  71.7 0.1 copy.69
  72.0 0.1 copy.69
  72.3 0.1 copy.69
  72.4 0.1 copy.70
  72.6 0.1 copy.69
  72.9 0.1 copy.69
  73.2 0.1 copy.58
  73.6 0.6 copy.66
  74.2 81.1 %all-to-all-done = bf16[64,64,128]{2,0,1:T(8,128)(2,1)S(1)} async-done(((bf16[64,64,128]{2,0,1:T(8,128)(2,1)}), bf16[64,64,128]{2,0,1:T(8,128)(2,1)S(1)}, u32[]{:S(2)}, u32[]{:S(2)}) %all-to-all-start) | async-done | bytes 1048608 | tf_op jit(solution)/shard_map/all_to_all | solution.py:53
  155.2 2.1 %copy.49 = bf16[32,64,2,128]{3,2,1,0:T(2,128)(2,1)} copy(bf16[32,64,2,128]{3,1,2,0:T(8,128)(2,1)S(1)} %bitcast.69) | data formatting | bytes 2097152 | tf_op jit(solution)/shard_map/all_to_all | solution.py:53
  (57 shorter events, 2.3 us)
Async XLA Ops:
  0.6 51.8 %copy-start = (bf16[4,1024,128]{2,1,0:T(8,128)(2,1)S(1)}, bf16[4,1024,128]{2,1,0:T(8,128)(2,1)}, u32[]{:S(2)}) copy-start(bf16[4,1024,128]{2,1,0:T(8,128)(2,1)} %param.14) | copy-start | bytes 3145732
  4.3 46.4 %copy-start.3 = (bf16[8,4096]{1,0:T(8,128)(2,1)S(1)}, bf16[8,4096]{1,0:T(8,128)(2,1)}, u32[]{:S(2)}) copy-start(bf16[8,4096]{1,0:T(8,128)(2,1)} %param.12) | copy-start | bytes 196612
  4.3 46.5 %copy-start.5 = (s32[8]{0:T(128)S(1)}, s32[8]{0:T(128)}, u32[]{:S(2)}) copy-start(s32[8]{0:T(128)} %param.17) | copy-start | bytes 100
  4.3 150.9 %all-to-all-start = ((bf16[64,64,128]{2,0,1:T(8,128)(2,1)}), bf16[64,64,128]{2,0,1:T(8,128)(2,1)S(1)}, u32[]{:S(2)}, u32[]{:S(2)}) async-start(bf16[64,64,128]{2,0,1:T(8,128)(2,1)} %copy_select_fusion), calls=%async_computation | async-start | bytes 2097152 | tf_op jit(solution)/shard_map/all_to_all | solution.py:53
  50.8 0.9 copy-start.1
  50.8 2.5 %copy-start.4 = (bf16[4,1024,128]{2,1,0:T(8,128)(2,1)S(1)}, bf16[4,1024,128]{2,1,0:T(8,128)(2,1)}, u32[]{:S(2)}) copy-start(bf16[4,1024,128]{2,1,0:T(8,128)(2,1)} %param.15) | copy-start | bytes 3145732
  67.9 0.6 copy-start.2
  69.0 2.1 %slice-start = ((f32[8,10,128]{2,1,0:T(8,128)}), f32[8,8,128]{2,1,0:T(8,128)S(1)}, s32[]{:S(2)}) async-start(f32[8,10,128]{2,1,0:T(8,128)} %copy-done.2), calls=%async_computation.1 | async-start | bytes 65536 | tf_op jit(solution)/shard_map/slice | solution.py:20
where the time goes:
time: 158 us; the launch traced here: 157 us
  waiting for transfers between devices  81.1 us (51%)
  starting transfers between devices  46.4 us (29%)
  blocking collectives  14.3 us (9%)
  local copies, waits for them, and re-layouts  8.79 us (6%)
  other arithmetic  4.29 us (3%)
    all_to_all x1, waiting for transfers between devices, per_device(): lax.all_to_all(kept, 'seq', split_axis=1, concat_axis=0, tiled=True)  81.1 us
    all_to_all x1, starting transfers between devices, per_device(): lax.all_to_all(kept, 'seq', split_axis=1, concat_axis=0, tiled=True)  46.4 us
    all_gather x1, blocking collectives, collected_together(): both, at, found = (lax.all_gather(jnp.concatenate(lines), axis), 0, {})  14.3 us
  transfers between devices with their start and end apart: 1, of which 1 were waited for; matrix products, arithmetic and copies ran while one was open for 5% of the time, Pallas kernels for 0%

commit v1 on v0

--- a/solution.py
+++ b/solution.py
@@ -1,10 +1,87 @@
 import jax
 import jax.numpy as jnp
 from jax import lax
+from jax.experimental import pallas as pl
+from jax.experimental.pallas import tpu as pltpu
 from jax.sharding import PartitionSpec as P
 
 query_scale = 168.0 ** (-0.5)
 negative = -1e30
+
+
+def regroup_kernel(n, x_ref, o_ref, own, send_sem, recv_sems, up_sems, own_sem):
+    block = x_ref.shape[0]
+    me = lax.axis_index("seq")
+    v = lax.rem(me + n - 1, n)
+
+    def place(w):
+        return lax.rem(w + 1, n)
+
+    barrier = pltpu.get_barrier_semaphore()
+
+    @pl.when(v > 0)
+    def _():
+        pl.semaphore_wait(barrier, 1)
+
+    @pl.when(v < n - 1)
+    def _():
+        pl.semaphore_signal(barrier, inc=1, device_id={"seq": place(v + 1)})
+
+    fetch = pltpu.make_async_copy(x_ref.at[:, me], own, own_sem)
+    fetch.start()
+
+    def copy_to(w):
+        to = place(w)
+        return pltpu.make_async_remote_copy(
+            src_ref=x_ref.at[:, to],
+            dst_ref=o_ref.at[me],
+            send_sem=send_sem,
+            recv_sem=recv_sems.at[me],
+            device_id={"seq": to},
+        )
+
+    @pl.loop(0, v)
+    def _(w):
+        pl.semaphore_signal(up_sems.at[v], inc=1, device_id={"seq": place(w)})
+
+    @pl.loop(0, v)
+    def _(k):
+        copy_to(v - 1 - k).start()
+
+    @pl.loop(v + 1, n)
+    def _(w):
+        pl.semaphore_wait(up_sems.at[w], 1)
+        copy_to(w).start()
+
+    fetch.wait()
+    keep = pltpu.make_async_copy(own, o_ref.at[me], own_sem)
+    keep.start()
+
+    @pl.loop(1, n)
+    def _(k):
+        src = lax.rem(me + k, n)
+        pltpu.make_async_copy(o_ref.at[src], o_ref.at[src], recv_sems.at[src]).wait()
+
+    pltpu.make_async_copy(o_ref.at[pl.ds(0, n - 1)], o_ref.at[pl.ds(0, n - 1)], send_sem).wait()
+    keep.wait()
+
+
+def regroup(x, n):
+    block, _, rows, width = x.shape
+    return pl.pallas_call(
+        lambda *refs: regroup_kernel(n, *refs),
+        out_shape=jax.ShapeDtypeStruct((n, block, rows, width), x.dtype),
+        in_specs=[pl.BlockSpec(memory_space=pl.ANY)],
+        out_specs=pl.BlockSpec(memory_space=pl.ANY),
+        scratch_shapes=[
+            pltpu.VMEM((block, rows, width), x.dtype),
+            pltpu.SemaphoreType.DMA,
+            pltpu.SemaphoreType.DMA((n,)),
+            pltpu.SemaphoreType.REGULAR((n,)),
+            pltpu.SemaphoreType.DMA,
+        ],
+        compiler_params=pltpu.CompilerParams(collective_id=0, has_side_effects=True),
+    )(x)
 
 
 def collected_together(shard, axis):
@@ -45,12 +122,15 @@
 
 def per_device(prompt_kv, prompt_length, queries, new_kv, k_cache, v_cache, lengths, slots):
     block = prompt_kv.shape[0]
-    offset = (lax.axis_index("seq") * lax.axis_size("tp") + lax.axis_index("tp")) * block
-    position = offset + jnp.arange(block, dtype=jnp.int32)
-    kept = jnp.where(
-        (position < prompt_length[0])[:, None, None], prompt_kv, jnp.zeros_like(prompt_kv)
-    )
-    prompt_owned = lax.all_to_all(kept, "seq", split_axis=1, concat_axis=0, tiled=True)
+    n = lax.axis_size("seq")
+    rows_each = prompt_kv.shape[1] // n
+    width = prompt_kv.shape[2]
+    landed = regroup(prompt_kv.reshape(block, n, rows_each, width), n)
+    start = (jnp.arange(n, dtype=jnp.int32) * lax.axis_size("tp") + lax.axis_index("tp")) * block
+    position = start[:, None] + jnp.arange(block, dtype=jnp.int32)
+    live_prompt = (position < prompt_length[0])[:, :, None, None]
+    prompt_owned = jnp.where(live_prompt, landed, jnp.zeros_like(landed))
+    prompt_owned = prompt_owned.reshape(n * block, rows_each, width)
     resident = lengths.shape[0]
     pair_rows = k_cache.shape[0]
     span = k_cache.shape[1]

time: 158 us -> 169 us (1.070)
  Pallas kernels: 0 us -> 95.8 us
  waiting for transfers between devices: 81.1 us -> 0 us
  starting transfers between devices: 46.4 us -> 0 us
  blocking collectives: 14.3 us -> 54.2 us
  other arithmetic: 4.29 us -> 7.92 us
    pallas_call x0 -> x1, Pallas kernels: none -> 95.8 us  [regroup(): pl.pallas_call(lambda *refs: regroup_kernel(n, *refs), out_shape=jax.Shap...]
    all_to_all x1 -> x0, waiting for transfers between devices: 81.1 us -> none  [per_device(): lax.all_to_all(kept, 'seq', split_axis=1, concat_axis=0, tiled=True)]
    all_to_all x1 -> x0, starting transfers between devices: 46.4 us -> none  [per_device(): lax.all_to_all(kept, 'seq', split_axis=1, concat_axis=0, tiled=True)]
    all_gather x1, blocking collectives: 14.3 us -> 54.2 us  [collected_together(): both, at, found = (lax.all_gather(jnp.concatenate(lines), axis), 0, {})]
    select_n x1, other arithmetic: 2.94 us -> 6.49 us  [per_device(): prompt_owned = jnp.where(live_prompt, landed, jnp.zeros_like(landed))]
    all_to_all x1 -> x0, local copies, waits for them, and re-layouts: 2.05 us -> none  [per_device(): lax.all_to_all(kept, 'seq', split_axis=1, concat_axis=0, tiled=True)]
  transfers between devices with their start and end apart: 1 -> 0, of which waited for: 1 -> 0; matrix products, arithmetic and copies ran while one was open for 5% -> 0% of each run, Pallas kernels for 0% -> 0%
where the time goes in v1:
time: 169 us
  Pallas kernels  95.8 us (57%)
  blocking collectives  54.2 us (32%)
  local copies, waits for them, and re-layouts  8.47 us (5%)
  other arithmetic  7.92 us (5%)
    pallas_call x1, Pallas kernels, regroup(): pl.pallas_call(lambda *refs: regroup_kernel(n, *refs), out_shape=jax.Shap...  95.8 us
    all_gather x1, blocking collectives, collected_together(): both, at, found = (lax.all_gather(jnp.concatenate(lines), axis), 0, {})  54.2 us
    select_n x1, other arithmetic, per_device(): prompt_owned = jnp.where(live_prompt, landed, jnp.zeros_like(landed))  6.49 us

profile of v1, /device:TPU:33, one launch (start us, length us, event | category | flops | bytes accessed | tf_op | source)
XLA Modules:
  0.0 168.7 jit_solution(244365449146034695)
XLA Ops:
  1.4 0.6 copy-done.5
  2.1 0.2 select_reduce_fusion
  2.3 1.4 gather_fusion.2
  3.8 0.6 copy-done.1
  4.4 0.6 gather_fusion
  5.1 0.1 copy-done.3
  5.3 0.6 gather_fusion.1
  5.9 0.1 fusion.8
  6.0 0.1 copy.54
  6.1 0.5 fusion.23
  6.6 0.2 fusion.6
  6.8 0.3 fusion.4
  7.3 54.2 %all-gather.1 = f32[8,10,128]{2,1,0:T(8,128)S(1)} all-gather(f32[1,10,128]{2,1,0:T(8,128)S(1)} %maximum_bitcast_fusion), channel_id=2, replica_groups=mesh['groups'=2,'seq'=32,'tp'=8] {'tp'}, dimensions={0}, use_global_device_ids=true | all-gather | bytes 46080 | tf_op jit(solution)/shard_map/all_gather | solution.py:95
  61.5 0.6 copy-done.2
  62.1 0.1 copy.56
  62.2 0.1 slice_reduce_fusion
  62.4 0.1 copy.47
  62.5 0.1 copy.49
  62.6 0.1 copy.55
  62.7 0.1 slice_reduce_fusion.1
  62.9 0.1 copy.46
  63.1 0.4 slice-done
  63.4 2.1 %while.19 = (s32[]{:T(128)}, f32[4,2]{0,1:T(2,128)S(1)}, f32[4,2]{0,1:T(2,128)S(1)}, f32[4,2,128]{2,1,0:T(2,128)S(1)}, f32[8,4,2]{1,2,0:T(2,128)S(1)}, /*index=5...) while((s32[]{:T(128)}, f32[4,2]{0,1:T(2,128)S(1)}, ...), condition=%wide.region_4.5_spmd, body=%wide.region_3.4_spmd.sunk | while | flops 3125 | bytes 12879 | solution.py:111
  64.1 0.1 copy.62
  64.3 0.1 copy.62
  64.6 0.1 copy.62
  64.9 0.1 copy.62
  65.2 0.1 copy.62
  65.5 0.1 copy.52
  65.9 0.6 copy.59
  66.5 95.8 %shard_map.95 = bf16[32,64,2,128]{3,2,1,0:T(2,128)(2,1)} custom-call(bf16[64,32,2,128]{3,2,1,0:T(2,128)(2,1)} %bitcast.67), custom_call_target="tpu_custom_call" | custom-call | tf_op jit(solution)/shard_map/pallas_call | solution.py:71
  162.3 6.5 %broadcast_select_fusion = bf16[32,64,2,128]{3,2,1,0:T(2,128)(2,1)} fusion(bf16[32,64,2,128]{3,2,1,0:T(2,128)(2,1)} %shard_map.95, pred[32,64]{1,0:T(8,128)(4,1)S(1)} %add_compare_fusion), kind=kLoop, calls=%fused_computation.12 | loop fusion | flops 524288 | bytes 2099200 | tf_op jit(solution)/shard_map/jit(_where)/select_n | solution.py:132
  (56 shorter events, 2.6 us)
Async XLA Ops:
  0.6 5.5 %copy-start = (bf16[4,1024,128]{2,1,0:T(8,128)(2,1)S(1)}, bf16[4,1024,128]{2,1,0:T(8,128)(2,1)}, u32[]{:S(2)}) copy-start(bf16[4,1024,128]{2,1,0:T(8,128)(2,1)} %param.14) | copy-start | bytes 3145732
  1.4 0.7 copy-start.5
  3.8 0.7 copy-start.1
  4.4 0.8 copy-start.3
  4.4 2.4 %copy-start.4 = (bf16[4,1024,128]{2,1,0:T(8,128)(2,1)S(1)}, bf16[4,1024,128]{2,1,0:T(8,128)(2,1)}, u32[]{:S(2)}) copy-start(bf16[4,1024,128]{2,1,0:T(8,128)(2,1)} %param.15) | copy-start | bytes 3145732
  61.5 0.6 copy-start.2
  62.7 0.8 slice-start

commit v2 on v0

v2 whole, which is shorter than its diff:
```python
import jax
import jax.numpy as jnp
from jax import lax
from jax.experimental import pallas as pl
from jax.experimental.pallas import tpu as pltpu
from jax.sharding import PartitionSpec as P

query_scale = 168.0 ** (-0.5)
negative = -1e30
residue = 4


def signal(semaphore, axis, to):
    pl.semaphore_signal(semaphore, inc=1, device_id={axis: to})


def step_kernel(
    n,
    m,
    x_ref,
    length_ref,
    q_ref,
    new_ref,
    k_ref,
    v_ref,
    lengths_ref,
    slots_ref,
    out_ref,
    att_ref,
    land,
    kept,
    k_vm,
    v_vm,
    q_vm,
    new_vm,
    parts,
    send_sem,
    cross_sem,
    part_send_sem,
    own_sem,
    keep_sem,
    in_sems,
    recv_sems,
    part_sems,
    up_sems,
    token_sem,
    ring_sem,
    all_sem,
):
    me = lax.axis_index("seq")
    my = lax.axis_index("tp")
    half = n // 2
    place = lax.rem(me, half)
    gated = half - 1 - place
    block, _, rows, width = x_ref.shape

    barrier = pltpu.get_barrier_semaphore()

    @pl.when(me > 0)
    def _():
        pl.semaphore_wait(barrier, 1)

    @pl.when(me < n - 1)
    def _():
        signal(barrier, "seq", me + 1)

    @pl.when(me == 0)
    def _():
        @pl.loop(1, m)
        def _(t):
            signal(barrier, "tp", lax.rem(my + t, m))

    @pl.loop(0, me)
    def _(w):
        signal(up_sems.at[me], "seq", me - 1 - w)

    def copy_to(to, semaphore):
        return pltpu.make_async_remote_copy(
            src_ref=x_ref.at[:, to],
            dst_ref=land.at[me],
            send_sem=semaphore,
            recv_sem=recv_sems.at[me],
            device_id={"seq": to},
        )

    def send_down(low, high, semaphore):
        @pl.loop(low, high)
        def _(w):
            copy_to(w, semaphore).start()

    def send_up(low, high, semaphore):
        @pl.loop(low, high)
        def _(w):
            pl.semaphore_wait(up_sems.at[w], 1)
            copy_to(w, semaphore).start()

    def sent(count, semaphore):
        @pl.loop(0, count)
        def _(w):
            pltpu.make_async_copy(land.at[0], land.at[0], semaphore).wait()

    pairs, span = k_vm.shape[:2]
    resident = q_vm.shape[0]
    group = q_vm.shape[1] // width
    lines = pairs * group
    head = (me * pairs) // resident
    per_tile = new_vm.shape[1]
    new_row = lax.rem(head * 2, per_tile)
    new_tile = pl.multiple_of(head * 2 - new_row, per_tile)
    q_column = pl.multiple_of(head * (group * width), group * width)
    fetches = (
        pltpu.make_async_copy(x_ref.at[:, me], land.at[me], own_sem),
        pltpu.make_async_copy(k_ref, k_vm, in_sems.at[0]),
        pltpu.make_async_copy(v_ref, v_vm, in_sems.at[1]),
        pltpu.make_async_copy(q_ref.at[:, pl.ds(q_column, group * width)], q_vm, in_sems.at[2]),
        pltpu.make_async_copy(new_ref.at[:, pl.ds(new_tile, per_tile)], new_vm, in_sems.at[3]),
    )
    line = lax.broadcasted_iota(jnp.int32, (lines, 1), 0)

    def sequence_of(r):
        slot = lax.rem(me * pairs + r, resident)
        found = jnp.int32(0)
        for b in range(resident):
            found = found + jnp.where(slots_ref[b] == slot, b, 0)
        return found

    def chosen():
        which = lax.broadcasted_iota(jnp.int32, (resident, 1), 0)
        tile = lax.broadcasted_iota(jnp.int32, (per_tile, 1), 0)
        q_all = q_vm[...].astype(jnp.float32)
        query = jnp.zeros((lines, width), jnp.float32)
        own_key = jnp.zeros((lines, width), jnp.float32)
        own_value = jnp.zeros((lines, width), jnp.float32)
        live_len = jnp.zeros((lines, 1), jnp.int32)
        for r in range(pairs):
            b = sequence_of(r)
            one = jnp.sum(jnp.where(which == b, q_all, 0.0), axis=0, keepdims=True)
            for k in range(group):
                query = jnp.where(line == k * pairs + r, one[:, k * width : (k + 1) * width], query)
            mine = lax.rem(line, pairs) == r
            new = jnp.zeros((per_tile, width), jnp.float32)
            length = jnp.int32(0)
            for s in range(resident):
                new = jnp.where(b == s, new_vm[s].astype(jnp.float32), new)
                length = jnp.where(b == s, lengths_ref[s], length)
            key = jnp.sum(jnp.where(tile == new_row, new, 0.0), axis=0, keepdims=True)
            value = jnp.sum(jnp.where(tile == new_row + 1, new, 0.0), axis=0, keepdims=True)
            own_key = jnp.where(mine, key, own_key)
            own_value = jnp.where(mine, value, own_value)
            live_len = jnp.where(mine, length, live_len)
        own = jnp.sum(query * own_key, axis=1, keepdims=True) * query_scale
        return query, own, own_value, live_len

    def attend():
        for fetch in fetches[1:]:
            fetch.wait()
        query, _, _, live_len = chosen()
        query = query.astype(jnp.bfloat16)
        scores = jnp.zeros((lines, span), jnp.float32)
        for r in range(pairs):
            part = lax.dot_general(
                query, k_vm[r], (((1,), (1,)), ((), ())), preferred_element_type=jnp.float32
            )
            scores = jnp.where(lax.rem(line, pairs) == r, part, scores)
        position = my * span + lax.broadcasted_iota(jnp.int32, (lines, span), 1)
        live = position < live_len
        masked = jnp.where(live, scores * query_scale, negative)
        top = jnp.max(masked, axis=1, keepdims=True)
        weights = jnp.where(live, jnp.exp(masked - top), 0.0)
        total = jnp.sum(weights, axis=1, keepdims=True)
        rounded = weights.astype(jnp.bfloat16)
        summed = jnp.zeros((lines, width), jnp.float32)
        for r in range(pairs):
            part = jnp.dot(rounded, v_vm[r], preferred_element_type=jnp.float32)
            summed = jnp.where(lax.rem(line, pairs) == r, part, summed)
        parts[my, 0] = summed
        parts[my, 1] = jnp.broadcast_to(top, (lines, width))
        parts[my, 2] = jnp.broadcast_to(total, (lines, width))

    for fetch in fetches:
        fetch.start()

    @pl.when(me < half)
    def _():
        send_down(0, me, send_sem)

    @pl.when(me >= half)
    def _():
        send_down(0, place + 1, send_sem)
        send_down(half, me, send_sem)
        send_down(place + 1, half, cross_sem)

    attend()

    @pl.when(me < half)
    def _():
        send_up(me + 1, half, send_sem)
        send_up(half, half + place + 1, send_sem)

        @pl.when(place > 0)
        def _():
            pl.semaphore_wait(token_sem, 1)

        send_up(half + place + 1, n, cross_sem)
        sent(jnp.maximum(gated - residue, 0), cross_sem)

        @pl.when(place < half - 1)
        def _():
            signal(token_sem, "seq", me + 1)

    @pl.when(me >= half)
    def _():
        send_up(me + 1, n, send_sem)

    @pl.when(me == 0)
    def _():
        pl.semaphore_wait(barrier, m - 1)

        @pl.loop(1, m)
        def _(t):
            signal(ring_sem, "tp", lax.rem(my + t, m))

        pl.semaphore_wait(ring_sem, m - 1)

        @pl.loop(1, n)
        def _(w):
            signal(all_sem, "seq", w)

    @pl.when(me > 0)
    def _():
        pl.semaphore_wait(all_sem, 1)

    def part_to(t):
        return pltpu.make_async_remote_copy(
            src_ref=parts.at[my],
            dst_ref=parts.at[my],
            send_sem=part_send_sem,
            recv_sem=part_sems.at[my],
            device_id={"tp": lax.rem(my + t, m)},
        )

    @pl.loop(1, m)
    def _(t):
        part_to(t).start()

    @pl.loop(1, m)
    def _(t):
        other = lax.rem(my + t, m)
        pltpu.make_async_copy(parts.at[other], parts.at[other], part_sems.at[other]).wait()

    _, own, own_value, _ = chosen()
    overall = jnp.broadcast_to(own, (lines, width))
    for t in range(m):
        overall = jnp.maximum(overall, parts[t, 1])
    own_weight = jnp.exp(own - overall)
    summed = own_weight * own_value
    total = own_weight
    for t in range(m):
        scale = jnp.exp(parts[t, 1] - overall)
        summed = summed + parts[t, 0] * scale
        total = total + parts[t, 2] * scale
    att_ref[...] = summed / total

    def keep(s):
        start = (s * m + my) * block
        position = start + lax.broadcasted_iota(jnp.int32, (block, rows, width), 0)
        arrived = land[s].astype(jnp.float32)
        kept[s] = jnp.where(position < length_ref[0], arrived, 0.0).astype(kept.dtype)
        pltpu.make_async_copy(kept.at[s], out_ref.at[s], keep_sem).start()

    fetches[0].wait()
    keep(me)

    @pl.loop(1, n)
    def _(w):
        s = lax.rem(me + w, n)
        pltpu.make_async_copy(land.at[s], land.at[s], recv_sems.at[s]).wait()
        keep(s)

    sent(n - 1 - gated, send_sem)

    @pl.when(me < half)
    def _():
        sent(jnp.minimum(gated, residue), cross_sem)

    @pl.when(me >= half)
    def _():
        sent(gated, cross_sem)

    @pl.loop(1, m)
    def _(t):
        pltpu.make_async_copy(parts.at[0], parts.at[0], part_send_sem).wait()

    pltpu.make_async_copy(kept, out_ref, keep_sem).wait()


def finish_kernel(owned_ref, att_ref, out_ref, attended_ref, held, in_sems, out_sem):
    pieces = in_sems.shape[0]
    each = owned_ref.shape[0] // pieces
    pairs, lanes = attended_ref.shape
    width = att_ref.shape[1]

    def fetch(i):
        at = pl.ds(i * each, each)
        return pltpu.make_async_copy(owned_ref.at[at], held.at[at], in_sems.at[i])

    for i in range(pieces):
        fetch(i).start()
    for k in range(lanes // width):
        lines = att_ref[k * pairs : (k + 1) * pairs, :]
        attended_ref[:, k * width : (k + 1) * width] = lines.astype(attended_ref.dtype)
    for i in range(pieces):
        fetch(i).wait()
        at = pl.ds(i * each, each)
        pltpu.make_async_copy(held.at[at], out_ref.at[at], out_sem).start()
    pltpu.make_async_copy(held, out_ref, out_sem).wait()


def per_device(prompt_kv, prompt_length, queries, new_kv, k_cache, v_cache, lengths, slots):
    n = lax.axis_size("seq")
    m = lax.axis_size("tp")
    block, kv_rows, width = prompt_kv.shape
    rows = kv_rows // n
    resident, heads = new_kv.shape[:2]
    pairs, span, _ = k_cache.shape
    group = queries.shape[1] // (heads * width)
    lines = pairs * group
    anywhere = pl.BlockSpec(memory_space=pl.ANY)
    scalars = pl.BlockSpec(memory_space=pltpu.SMEM)
    vector = pl.BlockSpec(memory_space=pltpu.VMEM)
    dma, regular = pltpu.SemaphoreType.DMA, pltpu.SemaphoreType.REGULAR
    owned, attended = pl.pallas_call(
        lambda *refs: step_kernel(n, m, *refs),
        out_shape=(
            jax.ShapeDtypeStruct((n, block, rows, width), prompt_kv.dtype),
            jax.ShapeDtypeStruct((lines, width), jnp.float32),
        ),
        in_specs=[anywhere, scalars, anywhere, anywhere, anywhere, anywhere, scalars, scalars],
        out_specs=(anywhere, vector),
        scratch_shapes=[
            pltpu.VMEM((n, block, rows, width), prompt_kv.dtype),
            pltpu.VMEM((n, block, rows, width), prompt_kv.dtype),
            pltpu.VMEM(k_cache.shape, k_cache.dtype),
            pltpu.VMEM(v_cache.shape, v_cache.dtype),
            pltpu.VMEM((resident, group * width), queries.dtype),
            pltpu.VMEM((resident, 8, width), new_kv.dtype),
            pltpu.VMEM((m, 3, lines, width), jnp.float32),
            dma,
            dma,
            dma,
            dma,
            dma,
            dma((4,)),
            dma((n,)),
            dma((m,)),
            regular((n,)),
            regular,
            regular,
            regular,
        ],
        compiler_params=pltpu.CompilerParams(collective_id=0, has_side_effects=True),
    )(
        prompt_kv.reshape(block, n, rows, width),
        prompt_length,
        queries,
        new_kv.reshape(resident, heads * 2, width),
        k_cache,
        v_cache,
        lengths,
        slots,
    )
    return pl.pallas_call(
        finish_kernel,
        out_shape=(
            jax.ShapeDtypeStruct((n * block, rows, width), prompt_kv.dtype),
            jax.ShapeDtypeStruct((pairs, group * width), jnp.bfloat16),
        ),
        in_specs=[anywhere, vector],
        out_specs=(anywhere, vector),
        scratch_shapes=[pltpu.VMEM((n * block, rows, width), prompt_kv.dtype), dma((8,)), dma],
    )(owned.reshape(n * block, rows, width), attended)


def solution(mesh):
    in_specs = (
        P(("groups", "seq", "tp"), None, None),
        P("groups"),
        P("groups", None),
        P("groups", None, None, None),
        P(("groups", "seq"), "tp", None),
        P(("groups", "seq"), "tp", None),
        P("groups"),
        P("groups"),
    )
    out_specs = (P(("groups", "tp"), "seq", None), P(("groups", "seq"), None))
    return jax.shard_map(
        per_device, mesh=mesh, in_specs=in_specs, out_specs=out_specs, check_vma=False
    )
```

time: 158 us -> 130 us (0.82)
  the two profiles are of different devices: /device:TPU:33 before, /device:TPU:677 now
where the time goes in v2:
time: 130 us
  Pallas kernels  129 us (99%)
    pallas_call x1, Pallas kernels, per_device(): pl.pallas_call(lambda *refs: step_kernel(n, m, *refs), out_shape=(jax.Sha...  126 us
    pallas_call x1, Pallas kernels, per_device(): pl.pallas_call(finish_kernel, out_shape=(jax.ShapeDtypeStruct((n * block,...  3.28 us

profile of v2, /device:TPU:677, one launch (start us, length us, event | category | flops | bytes accessed | tf_op | source)
XLA Modules:
  0.0 130.2 jit_solution(5045379835538761615)
XLA Ops:
  1.3 125.6 %shard_map.95 = (bf16[32,64,2,128]{3,2,1,0:T(2,128)(2,1)}, f32[8,128]{1,0:T(8,128)}) custom-call(bf16[64,32,2,128]{3,2,1,0:T(2,128)(2,1)} %bitcast.3, s32[1]{0:T(128)S(6)} %copy.10.refs_1_, bf16[8,4096]{1,0:T(8,128)(2,1)} %refs_2_.1, bf16[8,32,128]{2,1,0:T(8,128)(2,1)} %bitcast.5, bf16[4,1024,128]{2,1,0:T(8,128)(2,1)} %refs_4_.1, ...), custom_call_target="tpu_custom_call" | custom-call | tf_op jit(solution)/shard_map/pallas_call | solution.py:332
  126.9 3.3 %shard_map.96 = (bf16[2048,2,128]{2,1,0:T(2,128)(2,1)}, bf16[4,256]{1,0:T(4,128)(2,1)}) custom-call(bf16[2048,2,128]{2,1,0:T(2,128)(2,1)} %bitcast.4, f32[8,128]{1,0:T(8,128)} %get-tuple-element.5.att_ref), custom_call_target="tpu_custom_call" | custom-call | tf_op jit(solution)/shard_map/pallas_call | solution.py:372

commit v3 on v2

--- a/solution.py
+++ b/solution.py
@@ -7,7 +7,8 @@
 
 query_scale = 168.0 ** (-0.5)
 negative = -1e30
-residue = 4
+leaders = ((0, 2), (1, 2), (2, 3), (3, 3), (4, 3), (5, 4), (6, 4), (7, 4))
+herald = None
 
 
 def signal(semaphore, axis, to):
@@ -37,6 +38,7 @@
     send_sem,
     cross_sem,
     part_send_sem,
+    length_sm,
     own_sem,
     keep_sem,
     in_sems,
@@ -44,6 +46,7 @@
     part_sems,
     up_sems,
     token_sem,
+    late_sem,
     ring_sem,
     all_sem,
 ):
@@ -51,16 +54,24 @@
     my = lax.axis_index("tp")
     half = n // 2
     place = lax.rem(me, half)
-    gated = half - 1 - place
+    late = (lax.axis_index("groups") == 0) & (my == 0)
+    first = late.astype(jnp.int32)
+    gated = jnp.where(me >= first, half - 1 - place, 0)
+    leading = jnp.bool_(False)
+    left = jnp.int32(0)
+    for leader, residue in leaders:
+        here = me == leader + first
+        leading = leading | here
+        left = jnp.where(here, residue, left)
     block, _, rows, width = x_ref.shape
 
     barrier = pltpu.get_barrier_semaphore()
 
-    @pl.when(me > 0)
+    @pl.when(me > first)
     def _():
         pl.semaphore_wait(barrier, 1)
 
-    @pl.when(me < n - 1)
+    @pl.when((me < n - 1) & ((me >= first) | late))
     def _():
         signal(barrier, "seq", me + 1)
 
@@ -70,9 +81,9 @@
         def _(t):
             signal(barrier, "tp", lax.rem(my + t, m))
 
-    @pl.loop(0, me)
+    @pl.loop(first, jnp.maximum(me, first))
     def _(w):
-        signal(up_sems.at[me], "seq", me - 1 - w)
+        signal(up_sems.at[me], "seq", first + me - 1 - w)
 
     def copy_to(to, semaphore):
         return pltpu.make_async_remote_copy(
@@ -93,6 +104,9 @@
         def _(w):
             pl.semaphore_wait(up_sems.at[w], 1)
             copy_to(w, semaphore).start()
+
+    def received(s):
+        pltpu.make_async_copy(land.at[s], land.at[s], recv_sems.at[s]).wait()
 
     def sent(count, semaphore):
         @pl.loop(0, count)
@@ -114,6 +128,7 @@
         pltpu.make_async_copy(v_ref, v_vm, in_sems.at[1]),
         pltpu.make_async_copy(q_ref.at[:, pl.ds(q_column, group * width)], q_vm, in_sems.at[2]),
         pltpu.make_async_copy(new_ref.at[:, pl.ds(new_tile, per_tile)], new_vm, in_sems.at[3]),
+        pltpu.make_async_copy(length_ref, length_sm, in_sems.at[4]),
     )
     line = lax.broadcasted_iota(jnp.int32, (lines, 1), 0)
 
@@ -182,34 +197,65 @@
 
     @pl.when(me < half)
     def _():
-        send_down(0, me, send_sem)
+        send_down(first, jnp.maximum(me, first), send_sem)
 
     @pl.when(me >= half)
     def _():
-        send_down(0, place + 1, send_sem)
-        send_down(half, me, send_sem)
+        send_down(first, place + 1, send_sem)
         send_down(place + 1, half, cross_sem)
 
     attend()
 
-    @pl.when(me < half)
+    @pl.when((me < half) & (me >= first))
     def _():
         send_up(me + 1, half, send_sem)
         send_up(half, half + place + 1, send_sem)
 
-        @pl.when(place > 0)
+    def greet():
+        signal(up_sems.at[me], "seq", 0)
+        copy_to(0, send_sem).start()
+
+    @pl.when(late & (me > 1))
+    def _():
+        pl.semaphore_wait(late_sem, 1)
+        greet()
+
+    @pl.when(me < first)
+    def _():
+        send_up(1, n, send_sem)
+
+    @pl.when((me < half) & (me >= first))
+    def _():
+        @pl.when(me > first)
         def _():
             pl.semaphore_wait(token_sem, 1)
 
-        send_up(half + place + 1, n, cross_sem)
-        sent(jnp.maximum(gated - residue, 0), cross_sem)
-
-        @pl.when(place < half - 1)
+        @pl.when(jnp.logical_not(leading) & (place < half - 1))
         def _():
             signal(token_sem, "seq", me + 1)
 
+        send_up(half + place + 1, n, cross_sem)
+
+        @pl.when(late & (me == 1))
+        def _():
+            pl.semaphore_wait(barrier, 1)
+
+            @pl.loop(2, n)
+            def _(w):
+                signal(late_sem, "seq", w)
+
+            greet()
+
+        @pl.when(leading)
+        def _():
+            sent(gated - left, cross_sem)
+            signal(token_sem, "seq", me + 1)
+
     @pl.when(me >= half)
     def _():
+        if herald is not None:
+            received(herald)
+        send_down(half, me, send_sem)
         send_up(me + 1, n, send_sem)
 
     @pl.when(me == 0)
@@ -265,7 +311,7 @@
         start = (s * m + my) * block
         position = start + lax.broadcasted_iota(jnp.int32, (block, rows, width), 0)
         arrived = land[s].astype(jnp.float32)
-        kept[s] = jnp.where(position < length_ref[0], arrived, 0.0).astype(kept.dtype)
+        kept[s] = jnp.where(position < length_sm[0], arrived, 0.0).astype(kept.dtype)
         pltpu.make_async_copy(kept.at[s], out_ref.at[s], keep_sem).start()
 
     fetches[0].wait()
@@ -274,18 +320,17 @@
     @pl.loop(1, n)
     def _(w):
         s = lax.rem(me + w, n)
-        pltpu.make_async_copy(land.at[s], land.at[s], recv_sems.at[s]).wait()
+        heard = False if herald is None else (me >= half) & (s == herald)
+
+        @pl.when(jnp.logical_not(heard))
+        def _():
+            received(s)
+
         keep(s)
 
     sent(n - 1 - gated, send_sem)
 
-    @pl.when(me < half)
-    def _():
-        sent(jnp.minimum(gated, residue), cross_sem)
-
-    @pl.when(me >= half)
-    def _():
-        sent(gated, cross_sem)
+    sent(jnp.where(leading, left, gated), cross_sem)
 
     @pl.loop(1, m)
     def _(t):
@@ -335,7 +380,7 @@
             jax.ShapeDtypeStruct((n, block, rows, width), prompt_kv.dtype),
             jax.ShapeDtypeStruct((lines, width), jnp.float32),
         ),
-        in_specs=[anywhere, scalars, anywhere, anywhere, anywhere, anywhere, scalars, scalars],
+        in_specs=[anywhere, anywhere, anywhere, anywhere, anywhere, anywhere, scalars, scalars],
         out_specs=(anywhere, vector),
         scratch_shapes=[
             pltpu.VMEM((n, block, rows, width), prompt_kv.dtype),
@@ -348,12 +393,14 @@
             dma,
             dma,
             dma,
+            pltpu.SMEM((1,), jnp.int32),
             dma,
             dma,
-            dma((4,)),
+            dma((5,)),
             dma((n,)),
             dma((m,)),
             regular((n,)),
+            regular,
             regular,
             regular,
             regular,

time: 130 us -> 134 us (1.031)
  the two profiles are of different devices: /device:TPU:677 before, /device:TPU:161 now
where the time goes in v3:
time: 134 us
  Pallas kernels  133 us (99%)
    pallas_call x1, Pallas kernels, per_device(): pl.pallas_call(lambda *refs: step_kernel(n, m, *refs), out_shape=(jax.Sha...  129 us
    pallas_call x1, Pallas kernels, per_device(): pl.pallas_call(finish_kernel, out_shape=(jax.ShapeDtypeStruct((n * block,...  3.28 us

profile of v3, /device:TPU:161, one launch (start us, length us, event | category | flops | bytes accessed | tf_op | source)
XLA Modules:
  0.0 134.0 jit_solution(1785346960961450875)
XLA Ops:
  1.3 129.5 %shard_map.95 = (bf16[32,64,2,128]{3,2,1,0:T(2,128)(2,1)}, f32[8,128]{1,0:T(8,128)}) custom-call(bf16[64,32,2,128]{3,2,1,0:T(2,128)(2,1)} %bitcast.3, s32[1]{0:T(128)S(6)} %copy.10.refs_1_, bf16[8,4096]{1,0:T(8,128)(2,1)} %refs_2_.1, bf16[8,32,128]{2,1,0:T(8,128)(2,1)} %bitcast.5, bf16[4,1024,128]{2,1,0:T(8,128)(2,1)} %refs_4_.1, ...), custom_call_target="tpu_custom_call" | custom-call | tf_op jit(solution)/shard_map/pallas_call | solution.py:377
  130.8 3.3 %shard_map.96 = (bf16[2048,2,128]{2,1,0:T(2,128)(2,1)}, bf16[4,256]{1,0:T(4,128)(2,1)}) custom-call(bf16[2048,2,128]{2,1,0:T(2,128)(2,1)} %bitcast.4, f32[8,128]{1,0:T(8,128)} %get-tuple-element.5.att_ref), custom_call_target="tpu_custom_call" | custom-call | tf_op jit(solution)/shard_map/pallas_call | solution.py:419

commit v4 on v3

--- a/solution.py
+++ b/solution.py
@@ -7,7 +7,7 @@
 
 query_scale = 168.0 ** (-0.5)
 negative = -1e30
-leaders = ((0, 2), (1, 2), (2, 3), (3, 3), (4, 3), (5, 4), (6, 4), (7, 4))
+leaders = ((0, 2), (1, 2), (2, 2), (3, 3), (4, 3), (5, 4), (6, 4), (7, 4))
 herald = None
 
 
@@ -339,26 +339,15 @@
     pltpu.make_async_copy(kept, out_ref, keep_sem).wait()
 
 
-def finish_kernel(owned_ref, att_ref, out_ref, attended_ref, held, in_sems, out_sem):
-    pieces = in_sems.shape[0]
-    each = owned_ref.shape[0] // pieces
+def finish_kernel(owned_ref, att_ref, out_ref, attended_ref, out_sem):
     pairs, lanes = attended_ref.shape
     width = att_ref.shape[1]
-
-    def fetch(i):
-        at = pl.ds(i * each, each)
-        return pltpu.make_async_copy(owned_ref.at[at], held.at[at], in_sems.at[i])
-
-    for i in range(pieces):
-        fetch(i).start()
+    write = pltpu.make_async_copy(owned_ref, out_ref, out_sem)
+    write.start()
     for k in range(lanes // width):
         lines = att_ref[k * pairs : (k + 1) * pairs, :]
         attended_ref[:, k * width : (k + 1) * width] = lines.astype(attended_ref.dtype)
-    for i in range(pieces):
-        fetch(i).wait()
-        at = pl.ds(i * each, each)
-        pltpu.make_async_copy(held.at[at], out_ref.at[at], out_sem).start()
-    pltpu.make_async_copy(held, out_ref, out_sem).wait()
+    write.wait()
 
 
 def per_device(prompt_kv, prompt_length, queries, new_kv, k_cache, v_cache, lengths, slots):
@@ -371,14 +360,15 @@
     group = queries.shape[1] // (heads * width)
     lines = pairs * group
     anywhere = pl.BlockSpec(memory_space=pl.ANY)
+    outside = pl.BlockSpec(memory_space=pltpu.HBM)
     scalars = pl.BlockSpec(memory_space=pltpu.SMEM)
     vector = pl.BlockSpec(memory_space=pltpu.VMEM)
     dma, regular = pltpu.SemaphoreType.DMA, pltpu.SemaphoreType.REGULAR
     owned, attended = pl.pallas_call(
         lambda *refs: step_kernel(n, m, *refs),
         out_shape=(
-            jax.ShapeDtypeStruct((n, block, rows, width), prompt_kv.dtype),
-            jax.ShapeDtypeStruct((lines, width), jnp.float32),
+            pltpu.VMEM((n, block, rows, width), prompt_kv.dtype),
+            pltpu.VMEM((lines, width), jnp.float32),
         ),
         in_specs=[anywhere, anywhere, anywhere, anywhere, anywhere, anywhere, scalars, scalars],
         out_specs=(anywhere, vector),
@@ -405,7 +395,9 @@
             regular,
             regular,
         ],
-        compiler_params=pltpu.CompilerParams(collective_id=0, has_side_effects=True),
+        compiler_params=pltpu.CompilerParams(
+            collective_id=0, has_side_effects=True, vmem_limit_bytes=60 * 2**20
+        ),
     )(
         prompt_kv.reshape(block, n, rows, width),
         prompt_length,
@@ -423,8 +415,9 @@
             jax.ShapeDtypeStruct((pairs, group * width), jnp.bfloat16),
         ),
         in_specs=[anywhere, vector],
-        out_specs=(anywhere, vector),
-        scratch_shapes=[pltpu.VMEM((n * block, rows, width), prompt_kv.dtype), dma((8,)), dma],
+        out_specs=(outside, vector),
+        scratch_shapes=[dma],
+        compiler_params=pltpu.CompilerParams(vmem_limit_bytes=16 * 2**20),
     )(owned.reshape(n * block, rows, width), attended)
 
 

time: 134 us -> 122 us (0.910)
  the two profiles are of different devices: /device:TPU:161 before, /device:TPU:548 now
where the time goes in v4:
time: 122 us; the launch traced here: 121 us
  Pallas kernels  120 us (98%)
  between operations  1.29 us (1%)
    pallas_call x1, Pallas kernels, per_device(): pl.pallas_call(lambda *refs: step_kernel(n, m, *refs), out_shape=(pltpu.V...  119 us

profile of v4, /device:TPU:548, one launch (start us, length us, event | category | flops | bytes accessed | tf_op | source)
XLA Modules:
  0.0 121.3 jit_solution(145374855861208446)
XLA Ops:
  1.3 118.5 %shard_map.95 = (bf16[32,64,2,128]{3,2,1,0:T(2,128)(2,1)S(1)}, f32[8,128]{1,0:T(8,128)S(1)}) custom-call(bf16[64,32,2,128]{3,2,1,0:T(2,128)(2,1)} %bitcast.4, s32[1]{0:T(128)S(6)} %copy.10.refs_1_, bf16[8,4096]{1,0:T(8,128)(2,1)} %refs_2_.1, bf16[8,32,128]{2,1,0:T(8,128)(2,1)} %bitcast.5, bf16[4,1024,128]{2,1,0:T(8,128)(2,1)} %refs_4_.1, ...), custom_call_target="tpu_custom_call" | custom-call | tf_op jit(solution)/shard_map/pallas_call | solution.py:367
  119.8 1.6 %shard_map.96 = (bf16[2048,2,128]{2,1,0:T(2,128)(2,1)}, bf16[4,256]{1,0:T(4,128)(2,1)}) custom-call(bf16[2048,2,128]{2,1,0:T(2,128)(2,1)S(1)} %bitcast.3, f32[8,128]{1,0:T(8,128)S(1)} %get-tuple-element.5.att_ref), custom_call_target="tpu_custom_call" | custom-call | tf_op jit(solution)/shard_map/pallas_call | solution.py:411

commit v5 on v4

--- a/solution.py
+++ b/solution.py
@@ -7,7 +7,7 @@
 
 query_scale = 168.0 ** (-0.5)
 negative = -1e30
-leaders = ((0, 2), (1, 2), (2, 2), (3, 3), (4, 3), (5, 4), (6, 4), (7, 4))
+leaders = ((0, 2), (1, 2), (2, 2), (3, 2), (4, 4), (5, 4), (6, 5), (7, 2), (8, 3))
 herald = None
 
 
@@ -30,6 +30,7 @@
     att_ref,
     land,
     kept,
+    held,
     k_vm,
     v_vm,
     q_vm,
@@ -38,6 +39,8 @@
     send_sem,
     cross_sem,
     part_send_sem,
+    pass_sem,
+    held_sems,
     length_sm,
     own_sem,
     keep_sem,
@@ -94,6 +97,39 @@
             device_id={"seq": to},
         )
 
+    def by(relay, to, slot):
+        return pltpu.make_async_remote_copy(
+            src_ref=x_ref.at[:, to],
+            dst_ref=held.at[slot],
+            send_sem=send_sem,
+            recv_sem=held_sems.at[slot],
+            device_id={"seq": relay},
+        )
+
+    def pass_on(source, to, slot):
+        return pltpu.make_async_remote_copy(
+            src_ref=held.at[slot],
+            dst_ref=land.at[source],
+            send_sem=pass_sem,
+            recv_sem=recv_sems.at[source],
+            device_id={"seq": to},
+        )
+
+    passes_down = (me > first) & (me <= half)
+    passes_up = (me >= half - 1 + first) & (me < n - 1)
+
+    def relay_down():
+        @pl.when(passes_down)
+        def _():
+            pltpu.make_async_copy(held.at[0], held.at[0], held_sems.at[0]).wait()
+            pass_on(me + half - 1, me - 1, 0).start()
+
+    def relay_up():
+        @pl.when(passes_up)
+        def _():
+            pltpu.make_async_copy(held.at[1], held.at[1], held_sems.at[1]).wait()
+            pass_on(me - half + 1, me + 1, 1).start()
+
     def send_down(low, high, semaphore):
         @pl.loop(low, high)
         def _(w):
@@ -201,7 +237,11 @@
 
     @pl.when(me >= half)
     def _():
-        send_down(first, place + 1, send_sem)
+        @pl.when(place >= first)
+        def _():
+            by(place + 1, place, 0).start()
+
+        send_down(first, jnp.maximum(place, first), send_sem)
         send_down(place + 1, half, cross_sem)
 
     attend()
@@ -209,7 +249,9 @@
     @pl.when((me < half) & (me >= first))
     def _():
         send_up(me + 1, half, send_sem)
-        send_up(half, half + place + 1, send_sem)
+        send_up(half, half + place, send_sem)
+        by(half + place - 1, half + place, 1).start()
+        pl.semaphore_wait(up_sems.at[half + place], 1)
 
     def greet():
         signal(up_sems.at[me], "seq", 0)
@@ -245,6 +287,9 @@
                 signal(late_sem, "seq", w)
 
             greet()
+
+        relay_down()
+        relay_up()
 
         @pl.when(leading)
         def _():
@@ -257,6 +302,8 @@
             received(herald)
         send_down(half, me, send_sem)
         send_up(me + 1, n, send_sem)
+        relay_down()
+        relay_up()
 
     @pl.when(me == 0)
     def _():
@@ -331,6 +378,7 @@
     sent(n - 1 - gated, send_sem)
 
     sent(jnp.where(leading, left, gated), cross_sem)
+    sent(passes_down.astype(jnp.int32) + passes_up.astype(jnp.int32), pass_sem)
 
     @pl.loop(1, m)
     def _(t):
@@ -375,6 +423,7 @@
         scratch_shapes=[
             pltpu.VMEM((n, block, rows, width), prompt_kv.dtype),
             pltpu.VMEM((n, block, rows, width), prompt_kv.dtype),
+            pltpu.VMEM((2, block, rows, width), prompt_kv.dtype),
             pltpu.VMEM(k_cache.shape, k_cache.dtype),
             pltpu.VMEM(v_cache.shape, v_cache.dtype),
             pltpu.VMEM((resident, group * width), queries.dtype),
@@ -383,6 +432,8 @@
             dma,
             dma,
             dma,
+            dma,
+            dma((2,)),
             pltpu.SMEM((1,), jnp.int32),
             dma,
             dma,

time: 122 us -> 120 us (0.984)
  the two profiles are of different devices: /device:TPU:548 before, /device:TPU:556 now
where the time goes in v5:
time: 120 us
  Pallas kernels  119 us (99%)
  between operations  1.29 us (1%)
    pallas_call x1, Pallas kernels, per_device(): pl.pallas_call(lambda *refs: step_kernel(n, m, *refs), out_shape=(pltpu.V...  117 us

profile of v5, /device:TPU:556, one launch (start us, length us, event | category | flops | bytes accessed | tf_op | source)
XLA Modules:
  0.0 120.0 jit_solution(8519196087359765106)
XLA Ops:
  1.3 117.1 %shard_map.95 = (bf16[32,64,2,128]{3,2,1,0:T(2,128)(2,1)S(1)}, f32[8,128]{1,0:T(8,128)S(1)}) custom-call(bf16[64,32,2,128]{3,2,1,0:T(2,128)(2,1)} %bitcast.4, s32[1]{0:T(128)S(6)} %copy.10.refs_1_, bf16[8,4096]{1,0:T(8,128)(2,1)} %refs_2_.1, bf16[8,32,128]{2,1,0:T(8,128)(2,1)} %bitcast.5, bf16[4,1024,128]{2,1,0:T(8,128)(2,1)} %refs_4_.1, ...), custom_call_target="tpu_custom_call" | custom-call | tf_op jit(solution)/shard_map/pallas_call | solution.py:415
  118.4 1.6 %shard_map.96 = (bf16[2048,2,128]{2,1,0:T(2,128)(2,1)}, bf16[4,256]{1,0:T(4,128)(2,1)}) custom-call(bf16[2048,2,128]{2,1,0:T(2,128)(2,1)S(1)} %bitcast.3, f32[8,128]{1,0:T(8,128)S(1)} %get-tuple-element.5.att_ref), custom_call_target="tpu_custom_call" | custom-call | tf_op jit(solution)/shard_map/pallas_call | solution.py:462

commit v6 on v5

--- a/solution.py
+++ b/solution.py
@@ -7,7 +7,7 @@
 
 query_scale = 168.0 ** (-0.5)
 negative = -1e30
-leaders = ((0, 2), (1, 2), (2, 2), (3, 2), (4, 4), (5, 4), (6, 5), (7, 2), (8, 3))
+leaders = ((0, 2), (1, 2), (2, 1), (3, 2), (4, 4), (5, 5), (6, 6), (7, 3), (8, 4))
 herald = None
 
 

time: 120 us -> 132 us (1.10)
  the two profiles are of different devices: /device:TPU:556 before, /device:TPU:161 now
where the time goes in v6:
time: 132 us
  Pallas kernels  131 us (99%)
    pallas_call x1, Pallas kernels, per_device(): pl.pallas_call(lambda *refs: step_kernel(n, m, *refs), out_shape=(pltpu.V...  129 us

profile of v6, /device:TPU:161, one launch (start us, length us, event | category | flops | bytes accessed | tf_op | source)
XLA Modules:
  0.0 131.9 jit_solution(14851557223154609277)
XLA Ops:
  1.3 129.1 %shard_map.95 = (bf16[32,64,2,128]{3,2,1,0:T(2,128)(2,1)S(1)}, f32[8,128]{1,0:T(8,128)S(1)}) custom-call(bf16[64,32,2,128]{3,2,1,0:T(2,128)(2,1)} %bitcast.4, s32[1]{0:T(128)S(6)} %copy.10.refs_1_, bf16[8,4096]{1,0:T(8,128)(2,1)} %refs_2_.1, bf16[8,32,128]{2,1,0:T(8,128)(2,1)} %bitcast.5, bf16[4,1024,128]{2,1,0:T(8,128)(2,1)} %refs_4_.1, ...), custom_call_target="tpu_custom_call" | custom-call | tf_op jit(solution)/shard_map/pallas_call | solution.py:415
  130.3 1.6 %shard_map.96 = (bf16[2048,2,128]{2,1,0:T(2,128)(2,1)}, bf16[4,256]{1,0:T(4,128)(2,1)}) custom-call(bf16[2048,2,128]{2,1,0:T(2,128)(2,1)S(1)} %bitcast.3, f32[8,128]{1,0:T(8,128)S(1)} %get-tuple-element.5.att_ref), custom_call_target="tpu_custom_call" | custom-call | tf_op jit(solution)/shard_map/pallas_call | solution.py:462
